TPU v7x, 32 devices: a whole 2x2x4 slice. The times are simulated.
32 devices in a mesh: group: 2 (over x), lat: 16 (over z, y, core).
Axes of the slice: x: 2, y: 2, z: 4, core: 2. Of those that a mesh axis runs over, the one named last changes fastest.
Arguments:
- grid_values: bfloat16 [224, 1440, 256], P(('group', 'lat')), parts along dimension 0, may hold values from -630 to 630
- lat_counts: int32 [16], replicated, may hold values from 1 to 7, 96 in all
- owner_wavenumber: int32 [384], replicated, may hold values from 0 to 383, each once
- legendre: bfloat16 [384, 96, 384], P('lat'), may hold values from -0.625 to 0.625
- quad_weight: float32 [96], replicated, may hold values from 0.3 to 3
- spectral_gain: float32 [384, 256], replicated, may hold values from 0.3 to 3
- channel_mix: bfloat16 [256, 256], replicated, may hold values from -0.375 to 0.375
Outputs:
- grid_output: bfloat16 [224, 1440, 256], P(('group', 'lat')), parts along dimension 0
There are 2 independent parts, one for each index of `group`. A program takes and returns all parts, laid end to end along the dimension named above; an argument that names none is the same for every part. Nothing has to cross between parts.
Inputs may be any that keep to these rules, and one draw needn't show every extreme that they name: `lat_counts`: some device has all 7 slots live. `owner_wavenumber`: each wavenumber appears once; device i of lat owns wavenumber slots i * 24 to (i + 1) * 24 - 1.
All inputs are finite; a program needn't handle non-finite values.
Results may differ from a plain program's by a relative error of at most 0.0095.
Values may be sent and summed in bfloat16 or wider, within the bound.
No kernel may reach another device: no remote copies, remote signals or barrier semaphores. Data moves between devices by JAX's collectives and lax.ppermute only.
A program may use at most 64 MiB of HBM per device.

v0:
```python
import math
import jax
import jax.numpy as jnp
from jax import lax
from jax.sharding import PartitionSpec as P


def live_slots(lat_counts, slot_count, live_total):
    devices = lat_counts.shape[0]
    starts = jnp.cumsum(lat_counts) - lat_counts
    device_ids = jnp.arange(devices, dtype=jnp.int32)
    slot_ids = jnp.arange(devices * slot_count, dtype=jnp.int32)
    holder = slot_ids // slot_count
    within = slot_ids - holder * slot_count
    holder_hot = holder[:, None] == device_ids[None, :]
    holder_count = jnp.sum(jnp.where(holder_hot, lat_counts[None, :], 0), axis=1)
    holder_start = jnp.sum(jnp.where(holder_hot, starts[None, :], 0), axis=1)
    slot_valid = within < holder_count
    slot_live = jnp.where(slot_valid, holder_start + within, 0)
    live_ids = jnp.arange(live_total, dtype=jnp.int32)
    reached = (starts[None, :] <= live_ids[:, None]).astype(jnp.int32)
    source = jnp.sum(reached, axis=1) - 1
    source_hot = source[:, None] == device_ids[None, :]
    source_start = jnp.sum(jnp.where(source_hot, starts[None, :], 0), axis=1)
    live_slot = source * slot_count + live_ids - source_start
    return (slot_valid, slot_live, live_slot)


def wave_angles(wave_list, longitudes):
    points = jnp.arange(longitudes, dtype=jnp.int32)
    phase = wave_list[:, None] * points[None, :] % longitudes
    return phase.astype(jnp.float32) * (2.0 * math.pi / longitudes)


def forward_table(wave_list, longitudes):
    angle = wave_angles(wave_list, longitudes)
    factor = 1.0 / math.sqrt(longitudes)
    return jnp.stack([jnp.cos(angle) * factor, -jnp.sin(angle) * factor], axis=1).astype(
        jnp.bfloat16
    )


def inverse_table(wave_list, longitudes):
    angle = wave_angles(wave_list, longitudes)
    factor = 1.0 / math.sqrt(longitudes)
    doubled = jnp.where(wave_list > 0, 2.0, 1.0).astype(jnp.float32)[:, None] * factor
    return jnp.stack([jnp.cos(angle) * doubled, -jnp.sin(angle) * doubled], axis=1).astype(
        jnp.bfloat16
    )


def body(
    grid_values, lat_counts, owner_wavenumber, legendre, quad_weight, spectral_gain, channel_mix
):
    slot_count, longitudes, channels = grid_values.shape
    my_index = lax.axis_index("lat")
    wave_count = owner_wavenumber.shape[0]
    wave_share, live_total, degrees = legendre.shape
    slot_valid, slot_live, live_slot = live_slots(lat_counts, slot_count, live_total)
    local_valid = lax.dynamic_slice_in_dim(slot_valid, my_index * slot_count, slot_count)
    row_weight = local_valid.astype(jnp.float32)[:, None, None]
    widened = grid_values.astype(jnp.float32) * row_weight
    totals = lax.psum(
        (jnp.sum(widened, axis=(0, 1)), jnp.sum(widened * widened, axis=(0, 1))), "lat"
    )
    points = live_total * longitudes
    channel_mean = totals[0] / points
    variance = totals[1] / points - channel_mean * channel_mean
    normed = (
        (grid_values.astype(jnp.float32) - channel_mean) * lax.rsqrt(variance + 1e-05) * row_weight
    ).astype(jnp.bfloat16)
    forward_flat = forward_table(owner_wavenumber, longitudes).reshape(2 * wave_count, longitudes)
    spectra = jnp.einsum("skc,qk->sqc", normed, forward_flat, preferred_element_type=jnp.float32)
    spectra = spectra.astype(jnp.bfloat16).reshape(slot_count, wave_count, 2, normed.shape[2])
    received = lax.all_to_all(spectra, "lat", split_axis=1, concat_axis=0, tiled=True)
    own_waves = lax.dynamic_slice_in_dim(owner_wavenumber, my_index * wave_share, wave_share)
    degree_mask = (jnp.arange(degrees, dtype=jnp.int32)[None, :] >= own_waves[:, None]).astype(
        jnp.float32
    )
    gathered = jnp.take(received, live_slot, axis=0)
    weighted = (gathered.astype(jnp.float32) * quad_weight[:, None, None, None]).astype(
        jnp.bfloat16
    )
    coefficient = jnp.einsum(
        "rgl,grtc->rltc", legendre, weighted, preferred_element_type=jnp.float32
    )
    filtered = (
        coefficient * degree_mask[:, :, None, None] * spectral_gain[None, :, None, :]
    ).astype(jnp.bfloat16)
    mixed = jnp.dot(filtered.reshape(-1, channels), channel_mix, preferred_element_type=jnp.float32)
    mixed = mixed.astype(jnp.bfloat16).reshape(wave_share, degrees, 2, channels)
    synthesis = jnp.einsum(
        "rgl,rltc->grtc", legendre, mixed, preferred_element_type=jnp.float32
    ).astype(jnp.bfloat16)
    outgoing = jnp.where(
        slot_valid[:, None, None, None],
        jnp.take(synthesis, slot_live, axis=0),
        jnp.zeros((), jnp.bfloat16),
    )
    inverse_flat = inverse_table(owner_wavenumber, longitudes).reshape(2 * wave_count, longitudes)
    returned = lax.all_to_all(outgoing, "lat", split_axis=0, concat_axis=1, tiled=True)
    flat_back = returned.reshape(slot_count, 2 * wave_count, returned.shape[3])
    return jnp.einsum(
        "sqc,qk->skc", flat_back, inverse_flat, preferred_element_type=jnp.float32
    ).astype(jnp.bfloat16)


def solution(mesh):
    return jax.shard_map(
        body,
        mesh=mesh,
        in_specs=(P(("group", "lat"), None, None), P(), P(), P("lat", None, None), P(), P(), P()),
        out_specs=P(("group", "lat"), None, None),
        check_vma=False,
    )
```

profile of v0, /device:TPU:15, one launch (start us, length us, event | category | flops | bytes accessed | tf_op | source)
XLA Modules:
  0.0 337.3 jit_solution(7146616504685830470)
XLA Ops:
  2.4 10.7 %multiply_convert_fusion.4 = (bf16[384,1,1440]{0,2,1:T(8,128)(2,1)S(1)}, bf16[384,1,1440]{0,2,1:T(8,128)(2,1)S(1)}, bf16[384,1,1440]{0,2,1:T(8,128)(2,1)S(1)}, bf16[384,1,1440]{0,2,1:T(8,128)(2,1)S(1)}) fusion(f32[384]{0:T(512)S(1)} %select_multiply_fusion, s32[384]{0:T(512)} %param.9), kind=kLoop, calls=%fused_computation.36 | loop fusion | flops 9953280 | bytes 4426752 | tf_op jit(solution)/shard_map/convert.2
  15.6 6.8 %copy.58 = bf16[384,2,1440]{2,1,0:T(2,128)(2,1)} copy(bf16[384,2,1440]{0,2,1:T(8,128)(2,1)} %get-tuple-element.20) | data formatting | bytes 4423680 | tf_op jit(solution)/shard_map/stack | solution.py:38
  22.4 6.0 %convert_element_type.92 = bf16[768,1440]{1,0:T(8,128)(2,1)} reshape(bf16[384,2,1440]{2,1,0:T(2,128)(2,1)} %copy.58) | data formatting | bytes 4423680 | tf_op jit(solution)/shard_map/convert_element_type | solution.py:38
  28.6 4.8 %fusion.2 = (f32[256]{0:T(256)S(1)}, f32[256]{0:T(256)S(1)}) fusion(bf16[7,1440,256]{2,1,0:T(8,128)(2,1)} %param.7, f32[7]{0:T(128)S(1)} %dynamic-slice_convert_fusion), kind=kLoop, calls=%fused_computation.8 | loop fusion | flops 12901888 | bytes 5163036 | tf_op jit(solution)/shard_map/reduce_sum | solution.py:64
  33.4 21.9 %all-reduce = (f32[256]{0:T(256)S(1)}, f32[256]{0:T(256)S(1)}) all-reduce(f32[256]{0:T(256)S(1)} %get-tuple-element.6, f32[256]{0:T(256)S(1)} %get-tuple-element.5), channel_id=1, replica_groups=mesh['group'=2,'lat'=16] {'lat'}, use_global_device_ids=true, to_apply=%region_8.9 | all-reduce | flops 512 | bytes 4096 | tf_op jit(solution)/shard_map/psum | solution.py:63
  55.4 9.3 %convert_bitcast_fusion.1 = bf16[7,768,256]{2,1,0:T(8,128)(2,1)} fusion(bf16[7,1440,256]{2,1,0:T(8,128)(2,1)} %param.7, f32[256]{0:T(256)S(1)} %get-tuple-element.16, f32[256]{0:T(256)S(1)} %get-tuple-element.15, f32[7]{0:T(128)S(1)} %dynamic-slice_convert_fusion, bf16[768,1440]{1,0:T(8,128)(2,1)} %convert_element_type.92), kind=kOutput, calls=%fused_computation.23 | convolution fusion | flops 3977895936 | bytes 10127388 | tf_op jit(solution)/shard_map/skc,qk->sqc/dot_general | solution.py:73
  64.6 6.5 %reshape.389 = bf16[7,384,2,256]{3,2,1,0:T(2,128)(2,1)} reshape(bf16[7,768,256]{2,1,0:T(8,128)(2,1)} %convert_bitcast_fusion.1) | data formatting | bytes 5505024 | tf_op jit(solution)/shard_map/reshape | solution.py:74
  71.1 5.2 %copy.60 = bf16[7,384,2,256]{3,2,0,1:T(2,128)(2,1)} copy(bf16[7,384,2,256]{3,2,1,0:T(2,128)(2,1)} %reshape.389) | data formatting | bytes 5505024 | tf_op jit(solution)/shard_map/reshape | solution.py:74
  76.3 16.8 %all-to-all-start = ((bf16[7,384,2,256]{3,2,0,1:T(2,128)(2,1)}), bf16[7,384,2,256]{3,2,0,1:T(2,128)(2,1)}, u32[]{:S(2)}, u32[]{:S(2)}) async-start(bf16[7,384,2,256]{3,2,0,1:T(2,128)(2,1)} %copy.60), calls=%async_computation | async-start | bytes 5505024 | tf_op jit(solution)/shard_map/all_to_all | solution.py:75
  94.4 60.3 %all-to-all-done = bf16[7,384,2,256]{3,2,0,1:T(2,128)(2,1)} async-done(((bf16[7,384,2,256]{3,2,0,1:T(2,128)(2,1)}), bf16[7,384,2,256]{3,2,0,1:T(2,128)(2,1)}, u32[]{:S(2)}, u32[]{:S(2)}) %all-to-all-start) | async-done | bytes 2752544 | tf_op jit(solution)/shard_map/all_to_all | solution.py:75
  158.6 4.0 %gather_fusion = bf16[96,24,2,256]{3,1,2,0:T(8,128)(2,1)} fusion(bf16[112,24,2,256]{3,1,2,0:T(8,128)(2,1)} %bitcast.59, s32[1024]{0:T(1024)S(1)} %pad_clamp_fusion.1), kind=kCustom, calls=%fused_computation | custom fusion | bytes 4718976 | tf_op jit(solution)/shard_map/jit(_take)/gather | solution.py:80
  165.0 6.1 %fusion = bf16[24,384,2,256]{1,3,2,0:T(8,128)(2,1)} fusion(f32[384,256]{0,1:T(8,128)S(1)} %copy.64, f32[24,384]{1,0:T(8,128)S(1)} %fusion.31, bf16[96,24,2,256]{3,1,2,0:T(8,128)(2,1)S(1)} %multiply_convert_fusion, bf16[24,96,384]{2,1,0:T(8,128)(2,1)S(1)} %copy-done), kind=kOutput, calls=%fused_computation.4 | convolution fusion | flops 920125440 | bytes 13996032 | tf_op jit(solution)/shard_map/rgl,grtc->rltc/dot_general | solution.py:84
  171.1 23.6 %copy.65 = bf16[24,384,2,256]{3,2,1,0:T(2,128)(2,1)} copy(bf16[24,384,2,256]{1,3,2,0:T(8,128)(2,1)} %fusion) | data formatting | bytes 18874368 | tf_op jit(solution)/shard_map/convert_element_type | solution.py:89
  194.7 14.6 %reshape.390 = bf16[18432,256]{1,0:T(8,128)(2,1)} reshape(bf16[24,384,2,256]{3,2,1,0:T(2,128)(2,1)} %copy.65) | data formatting | bytes 18874368 | tf_op jit(solution)/shard_map/reshape | solution.py:90
  209.3 9.9 %convolution_convert_fusion = bf16[18432,256]{1,0:T(8,128)(2,1)} fusion(bf16[18432,256]{1,0:T(8,128)(2,1)} %reshape.390, bf16[256,256]{1,0:T(8,128)(2,1)S(1)} %copy-done.2), kind=kOutput, calls=%fused_computation.2 | convolution fusion | flops 2420637696 | bytes 19005440 | tf_op jit(solution)/shard_map/dot_general | solution.py:90
  219.2 14.6 %reshape.391 = bf16[24,384,2,256]{3,2,1,0:T(2,128)(2,1)} reshape(bf16[18432,256]{1,0:T(8,128)(2,1)} %convolution_convert_fusion) | data formatting | bytes 18874368 | tf_op jit(solution)/shard_map/reshape | solution.py:91
  233.8 5.6 %convert_bitcast_fusion.2 = bf16[96,24,2,256]{3,0,2,1:T(8,128)(2,1)S(1)} fusion(bf16[24,384,2,256]{3,2,1,0:T(2,128)(2,1)} %reshape.391, bf16[24,96,384]{2,1,0:T(8,128)(2,1)S(1)} %copy-done), kind=kOutput, calls=%fused_computation.27 | convolution fusion | flops 907149312 | bytes 13565952 | tf_op jit(solution)/shard_map/rgl,rltc->grtc/dot_general | solution.py:92
  249.4 4.8 %all-to-all-start.1 = ((bf16[112,24,2,256]{3,1,2,0:T(8,128)(2,1)}), bf16[112,24,2,256]{3,1,2,0:T(8,128)(2,1)}, u32[]{:S(2)}, u32[]{:S(2)}) async-start(bf16[112,24,2,256]{3,1,2,0:T(8,128)(2,1)} %select_select_fusion), calls=%async_computation.1 | async-start | bytes 5505024 | tf_op jit(solution)/shard_map/all_to_all | solution.py:101
  254.2 6.9 %copy.56 = bf16[384,2,1440]{2,1,0:T(2,128)(2,1)} copy(bf16[384,2,1440]{0,2,1:T(8,128)(2,1)} %get-tuple-element.19) | data formatting | bytes 4423680 | tf_op jit(solution)/shard_map/stack | solution.py:47
  261.1 6.0 %convert_element_type.90 = bf16[768,1440]{1,0:T(8,128)(2,1)} reshape(bf16[384,2,1440]{2,1,0:T(2,128)(2,1)} %copy.56) | data formatting | bytes 4423680 | tf_op jit(solution)/shard_map/convert_element_type | solution.py:47
  267.1 48.7 %all-to-all-done.1 = bf16[112,24,2,256]{3,1,2,0:T(8,128)(2,1)} async-done(((bf16[112,24,2,256]{3,1,2,0:T(8,128)(2,1)}), bf16[112,24,2,256]{3,1,2,0:T(8,128)(2,1)}, u32[]{:S(2)}, u32[]{:S(2)}) %all-to-all-start.1) | async-done | bytes 2752544 | tf_op jit(solution)/shard_map/all_to_all | solution.py:101
  315.7 5.8 %copy.68 = bf16[7,16,24,2,256]{4,3,2,1,0:T(2,128)(2,1)} copy(bf16[7,16,24,2,256]{4,2,3,0,1:T(8,128)(2,1)} %bitcast.18) | data formatting | bytes 5505024 | tf_op jit(solution)/shard_map/all_to_all | solution.py:101
  321.5 6.8 %reshape.392 = bf16[7,768,256]{2,1,0:T(8,128)(2,1)} reshape(bf16[7,16,24,2,256]{4,3,2,1,0:T(2,128)(2,1)} %copy.68) | data formatting | bytes 5505024 | tf_op jit(solution)/shard_map/reshape | solution.py:102
  328.3 9.1 %convert_bitcast_fusion = bf16[7,1440,256]{2,1,0:T(8,128)(2,1)} fusion(bf16[7,768,256]{2,1,0:T(8,128)(2,1)} %reshape.392, bf16[768,1440]{1,0:T(8,128)(2,1)} %convert_element_type.90), kind=kOutput, calls=%fused_computation.16 | convolution fusion | flops 3966197760 | bytes 10125312 | tf_op jit(solution)/shard_map/sqc,qk->skc/dot_general | solution.py:103
  (38 shorter events, 22.6 us)
Async XLA Ops:
  0.0 165.0 %copy-start = (bf16[24,96,384]{2,1,0:T(8,128)(2,1)S(1)}, bf16[24,96,384]{2,1,0:T(8,128)(2,1)}, u32[]{:S(2)}) copy-start(bf16[24,96,384]{2,1,0:T(8,128)(2,1)} %param.10) | copy-start | bytes 5308420
  22.4 6.0 %copy-start.3 = (s32[16]{0:T(128)S(1)}, s32[16]{0:T(128)}, u32[]{:S(2)}) copy-start(s32[16]{0:T(128)} %param.8) | copy-start | bytes 196
  76.3 17.5 %copy-start.1 = (f32[384,256]{1,0:T(8,128)S(1)}, f32[384,256]{1,0:T(8,128)}, u32[]{:S(2)}) copy-start(f32[384,256]{1,0:T(8,128)} %param.12) | copy-start | bytes 1179652
  76.3 78.3 %all-to-all-start = ((bf16[7,384,2,256]{3,2,0,1:T(2,128)(2,1)}), bf16[7,384,2,256]{3,2,0,1:T(2,128)(2,1)}, u32[]{:S(2)}, u32[]{:S(2)}) async-start(bf16[7,384,2,256]{3,2,0,1:T(2,128)(2,1)} %copy.60), calls=%async_computation | async-start | bytes 5505024 | tf_op jit(solution)/shard_map/all_to_all | solution.py:75
  158.6 4.0 %copy-start.4 = (f32[96]{0:T(128)S(1)}, f32[96]{0:T(128)}, u32[]{:S(2)}) copy-start(f32[96]{0:T(128)} %param.11) | copy-start | bytes 1156
  194.7 14.6 %copy-start.2 = (bf16[256,256]{1,0:T(8,128)(2,1)S(1)}, bf16[256,256]{1,0:T(8,128)(2,1)}, u32[]{:S(2)}) copy-start(bf16[256,256]{1,0:T(8,128)(2,1)} %param.13) | copy-start | bytes 393220
  249.4 66.3 %all-to-all-start.1 = ((bf16[112,24,2,256]{3,1,2,0:T(8,128)(2,1)}), bf16[112,24,2,256]{3,1,2,0:T(8,128)(2,1)}, u32[]{:S(2)}, u32[]{:S(2)}) async-start(bf16[112,24,2,256]{3,1,2,0:T(8,128)(2,1)} %select_select_fusion), calls=%async_computation.1 | async-start | bytes 5505024 | tf_op jit(solution)/shard_map/all_to_all | solution.py:101
where the time goes:
time: 340 us; the launch traced here: 337 us
  local copies, waits for them, and re-layouts  119 us (35%)
  waiting for transfers between devices  109 us (32%)
  matrix products  39.9 us (12%)
  other arithmetic  25.5 us (8%)
  blocking collectives  21.9 us (6%)
  starting transfers between devices  21.5 us (6%)
    all_to_all x1, waiting for transfers between devices, body(): lax.all_to_all(spectra, 'lat', split_axis=1, concat_axis=0, tiled=True)  60.3 us
    all_to_all x1, waiting for transfers between devices, body(): lax.all_to_all(outgoing, 'lat', split_axis=0, concat_axis=1, tiled=True)  48.7 us
    convert_element_type x1, local copies, waits for them, and re-layouts, body(): filtered = (coefficient * degree_mask[:, :, None, None] * spectral_gain[N...  23.6 us
    psum x1, blocking collectives, body(): lax.psum((jnp.sum(widened, axis=(0, 1)), jnp.sum(widened * widened, axis=...  21.9 us
    all_to_all x1, starting transfers between devices, body(): lax.all_to_all(spectra, 'lat', split_axis=1, concat_axis=0, tiled=True)  16.8 us
    reshape x1, local copies, waits for them, and re-layouts, body(): filtered.reshape(-1, channels)  14.6 us
    reshape x1, local copies, waits for them, and re-layouts, body(): mixed = mixed.astype(jnp.bfloat16).reshape(wave_share, degrees, 2, channels)  14.6 us
    reshape x2, local copies, waits for them, and re-layouts, body(): spectra.astype(jnp.bfloat16)  11.7 us
  transfers between devices with their start and end apart: 2, of which 2 were waited for; matrix products, arithmetic and copies ran while one was open for 4% of the time, Pallas kernels for 0%

commit v1 on v0

--- a/solution.py
+++ b/solution.py
@@ -72,7 +72,10 @@
     forward_flat = forward_table(owner_wavenumber, longitudes).reshape(2 * wave_count, longitudes)
     spectra = jnp.einsum("skc,qk->sqc", normed, forward_flat, preferred_element_type=jnp.float32)
     spectra = spectra.astype(jnp.bfloat16).reshape(slot_count, wave_count, 2, normed.shape[2])
-    received = lax.all_to_all(spectra, "lat", split_axis=1, concat_axis=0, tiled=True)
+    received = jnp.concatenate(
+        lax.all_to_all(jnp.stack(jnp.split(spectra, lax.axis_size("lat"), axis=1)), "lat", 0, 0),
+        axis=0,
+    )
     own_waves = lax.dynamic_slice_in_dim(owner_wavenumber, my_index * wave_share, wave_share)
     degree_mask = (jnp.arange(degrees, dtype=jnp.int32)[None, :] >= own_waves[:, None]).astype(
         jnp.float32

time: 340 us -> 362 us (1.065)
  local copies, waits for them, and re-layouts: 119 us -> 141 us
    unnamed x11 -> x26, local copies, waits for them, and re-layouts: 0.18 us -> 25.8 us
    reshape x2 -> x1, local copies, waits for them, and re-layouts: 11.7 us -> 6.53 us  [body(): spectra.astype(jnp.bfloat16)]
where the time goes in v1:
time: 362 us; the launch traced here: 359 us
  local copies, waits for them, and re-layouts  141 us (39%)
  waiting for transfers between devices  109 us (30%)
  matrix products  39.9 us (11%)
  other arithmetic  25.5 us (7%)
  blocking collectives  21.9 us (6%)
  starting transfers between devices  21.5 us (6%)
    all_to_all x1, waiting for transfers between devices, body(): lax.all_to_all(jnp.stack(jnp.split(spectra, lax.axis_size('lat'), axis=1)...  60.3 us
    all_to_all x1, waiting for transfers between devices, body(): lax.all_to_all(outgoing, 'lat', split_axis=0, concat_axis=1, tiled=True)  48.7 us
    unnamed x26, local copies, waits for them, and re-layouts  25.8 us
    convert_element_type x1, local copies, waits for them, and re-layouts, body(): filtered = (coefficient * degree_mask[:, :, None, None] * spectral_gain[N...  23.6 us
    psum x1, blocking collectives, body(): lax.psum((jnp.sum(widened, axis=(0, 1)), jnp.sum(widened * widened, axis=...  21.9 us
    all_to_all x1, starting transfers between devices, body(): lax.all_to_all(jnp.stack(jnp.split(spectra, lax.axis_size('lat'), axis=1)...  16.8 us
    reshape x1, local copies, waits for them, and re-layouts, body(): filtered.reshape(-1, channels)  14.6 us
    reshape x1, local copies, waits for them, and re-layouts, body(): mixed = mixed.astype(jnp.bfloat16).reshape(wave_share, degrees, 2, channels)  14.6 us
  transfers between devices with their start and end apart: 2, of which 2 were waited for; matrix products, arithmetic and copies ran while one was open for 4% of the time, Pallas kernels for 0%

profile of v1, /device:TPU:15, one launch (start us, length us, event | category | flops | bytes accessed | tf_op | source)
XLA Modules:
  0.0 359.3 jit_solution(7982414762533243867)
XLA Ops:
  2.4 10.7 %multiply_convert_fusion.4 = (bf16[384,1,1440]{0,2,1:T(8,128)(2,1)S(1)}, bf16[384,1,1440]{0,2,1:T(8,128)(2,1)S(1)}, bf16[384,1,1440]{0,2,1:T(8,128)(2,1)S(1)}, bf16[384,1,1440]{0,2,1:T(8,128)(2,1)S(1)}) fusion(f32[384]{0:T(512)S(1)} %select_multiply_fusion, s32[384]{0:T(512)} %param.9), kind=kLoop, calls=%fused_computation.36 | loop fusion | flops 9953280 | bytes 4426752 | tf_op jit(solution)/shard_map/convert.2
  15.6 6.8 %copy.34 = bf16[384,2,1440]{2,1,0:T(2,128)(2,1)} copy(bf16[384,2,1440]{0,2,1:T(8,128)(2,1)} %get-tuple-element.20) | data formatting | bytes 4423680 | tf_op jit(solution)/shard_map/stack | solution.py:38
  22.4 6.0 %convert_element_type.92 = bf16[768,1440]{1,0:T(8,128)(2,1)} reshape(bf16[384,2,1440]{2,1,0:T(2,128)(2,1)} %copy.34) | data formatting | bytes 4423680 | tf_op jit(solution)/shard_map/convert_element_type | solution.py:38
  28.6 4.8 %fusion.2 = (f32[256]{0:T(256)S(1)}, f32[256]{0:T(256)S(1)}) fusion(bf16[7,1440,256]{2,1,0:T(8,128)(2,1)} %param.7, f32[7]{0:T(128)S(1)} %dynamic-slice_convert_fusion), kind=kLoop, calls=%fused_computation.8 | loop fusion | flops 12901888 | bytes 5163036 | tf_op jit(solution)/shard_map/reduce_sum | solution.py:64
  33.4 21.9 %all-reduce = (f32[256]{0:T(256)S(1)}, f32[256]{0:T(256)S(1)}) all-reduce(f32[256]{0:T(256)S(1)} %get-tuple-element.6, f32[256]{0:T(256)S(1)} %get-tuple-element.5), channel_id=1, replica_groups=mesh['group'=2,'lat'=16] {'lat'}, use_global_device_ids=true, to_apply=%region_8.9 | all-reduce | flops 512 | bytes 4096 | tf_op jit(solution)/shard_map/psum | solution.py:63
  55.4 9.3 %convert_bitcast_fusion.1 = bf16[7,768,256]{2,1,0:T(8,128)(2,1)} fusion(bf16[7,1440,256]{2,1,0:T(8,128)(2,1)} %param.7, f32[256]{0:T(256)S(1)} %get-tuple-element.16, f32[256]{0:T(256)S(1)} %get-tuple-element.15, f32[7]{0:T(128)S(1)} %dynamic-slice_convert_fusion, bf16[768,1440]{1,0:T(8,128)(2,1)} %convert_element_type.92), kind=kOutput, calls=%fused_computation.23 | convolution fusion | flops 3977895936 | bytes 10127388 | tf_op jit(solution)/shard_map/skc,qk->sqc/dot_general | solution.py:73
  64.6 6.5 %reshape.392 = bf16[7,384,2,256]{3,2,1,0:T(2,128)(2,1)} reshape(bf16[7,768,256]{2,1,0:T(8,128)(2,1)} %convert_bitcast_fusion.1) | data formatting | bytes 5505024 | tf_op jit(solution)/shard_map/reshape | solution.py:74
  98.5 16.8 %all-to-all-start = ((bf16[16,7,24,2,256]{4,3,2,1,0:T(2,128)(2,1)}), bf16[16,7,24,2,256]{4,3,2,1,0:T(2,128)(2,1)}, u32[]{:S(2)}, u32[]{:S(2)}) async-start(bf16[16,7,24,2,256]{4,3,2,1,0:T(2,128)(2,1)} %fusion.31), calls=%async_computation | async-start | bytes 5505024 | tf_op jit(solution)/shard_map/all_to_all | solution.py:76
  116.5 60.3 %all-to-all-done = bf16[16,7,24,2,256]{4,3,2,1,0:T(2,128)(2,1)} async-done(((bf16[16,7,24,2,256]{4,3,2,1,0:T(2,128)(2,1)}), bf16[16,7,24,2,256]{4,3,2,1,0:T(2,128)(2,1)}, u32[]{:S(2)}, u32[]{:S(2)}) %all-to-all-start) | async-done | bytes 2752544 | tf_op jit(solution)/shard_map/all_to_all | solution.py:76
  180.6 4.0 %gather_fusion = bf16[96,24,2,256]{3,1,2,0:T(8,128)(2,1)} fusion(bf16[112,24,2,256]{3,1,2,0:T(8,128)(2,1)} %bitcast.119, s32[1024]{0:T(1024)S(1)} %pad_clamp_fusion.1), kind=kCustom, calls=%fused_computation | custom fusion | bytes 4718976 | tf_op jit(solution)/shard_map/jit(_take)/gather | solution.py:83
  186.9 6.1 %fusion = bf16[24,384,2,256]{1,3,2,0:T(8,128)(2,1)} fusion(f32[384,256]{0,1:T(8,128)S(1)} %copy.38, f32[24,384]{1,0:T(8,128)S(1)} %fusion.47, bf16[96,24,2,256]{3,1,2,0:T(8,128)(2,1)S(1)} %multiply_convert_fusion, bf16[24,96,384]{2,1,0:T(8,128)(2,1)S(1)} %copy-done), kind=kOutput, calls=%fused_computation.4 | convolution fusion | flops 920125440 | bytes 13996032 | tf_op jit(solution)/shard_map/rgl,grtc->rltc/dot_general | solution.py:87
  193.0 23.6 %copy.39 = bf16[24,384,2,256]{3,2,1,0:T(2,128)(2,1)} copy(bf16[24,384,2,256]{1,3,2,0:T(8,128)(2,1)} %fusion) | data formatting | bytes 18874368 | tf_op jit(solution)/shard_map/convert_element_type | solution.py:92
  216.6 14.6 %reshape.394 = bf16[18432,256]{1,0:T(8,128)(2,1)} reshape(bf16[24,384,2,256]{3,2,1,0:T(2,128)(2,1)} %copy.39) | data formatting | bytes 18874368 | tf_op jit(solution)/shard_map/reshape | solution.py:93
  231.2 9.9 %convolution_convert_fusion = bf16[18432,256]{1,0:T(8,128)(2,1)} fusion(bf16[18432,256]{1,0:T(8,128)(2,1)} %reshape.394, bf16[256,256]{1,0:T(8,128)(2,1)S(1)} %copy-done.2), kind=kOutput, calls=%fused_computation.2 | convolution fusion | flops 2420637696 | bytes 19005440 | tf_op jit(solution)/shard_map/dot_general | solution.py:93
  241.2 14.6 %reshape.395 = bf16[24,384,2,256]{3,2,1,0:T(2,128)(2,1)} reshape(bf16[18432,256]{1,0:T(8,128)(2,1)} %convolution_convert_fusion) | data formatting | bytes 18874368 | tf_op jit(solution)/shard_map/reshape | solution.py:94
  255.8 5.6 %convert_bitcast_fusion.2 = bf16[96,24,2,256]{3,0,2,1:T(8,128)(2,1)S(1)} fusion(bf16[24,384,2,256]{3,2,1,0:T(2,128)(2,1)} %reshape.395, bf16[24,96,384]{2,1,0:T(8,128)(2,1)S(1)} %copy-done), kind=kOutput, calls=%fused_computation.27 | convolution fusion | flops 907149312 | bytes 13565952 | tf_op jit(solution)/shard_map/rgl,rltc->grtc/dot_general | solution.py:95
  264.1 4.0 %gather_fusion.1 = bf16[112,24,2,256]{3,1,2,0:T(8,128)(2,1)} fusion(bf16[96,24,2,256]{3,1,2,0:T(8,128)(2,1)} %copy.41, s32[1024]{0:T(1024)S(1)} %pad_clamp_fusion), kind=kCustom, calls=%fused_computation.1 | custom fusion | bytes 5505472 | tf_op jit(solution)/shard_map/jit(_take)/gather | solution.py:100
  271.3 4.8 %all-to-all-start.1 = ((bf16[112,24,2,256]{3,1,2,0:T(8,128)(2,1)}), bf16[112,24,2,256]{3,1,2,0:T(8,128)(2,1)}, u32[]{:S(2)}, u32[]{:S(2)}) async-start(bf16[112,24,2,256]{3,1,2,0:T(8,128)(2,1)} %select_select_fusion), calls=%async_computation.1 | async-start | bytes 5505024 | tf_op jit(solution)/shard_map/all_to_all | solution.py:104
  276.1 6.9 %copy.32 = bf16[384,2,1440]{2,1,0:T(2,128)(2,1)} copy(bf16[384,2,1440]{0,2,1:T(8,128)(2,1)} %get-tuple-element.19) | data formatting | bytes 4423680 | tf_op jit(solution)/shard_map/stack | solution.py:47
  283.0 6.0 %convert_element_type.90 = bf16[768,1440]{1,0:T(8,128)(2,1)} reshape(bf16[384,2,1440]{2,1,0:T(2,128)(2,1)} %copy.32) | data formatting | bytes 4423680 | tf_op jit(solution)/shard_map/convert_element_type | solution.py:47
  289.0 48.7 %all-to-all-done.1 = bf16[112,24,2,256]{3,1,2,0:T(8,128)(2,1)} async-done(((bf16[112,24,2,256]{3,1,2,0:T(8,128)(2,1)}), bf16[112,24,2,256]{3,1,2,0:T(8,128)(2,1)}, u32[]{:S(2)}, u32[]{:S(2)}) %all-to-all-start.1) | async-done | bytes 2752544 | tf_op jit(solution)/shard_map/all_to_all | solution.py:104
  337.7 5.8 %copy.42 = bf16[7,16,24,2,256]{4,3,2,1,0:T(2,128)(2,1)} copy(bf16[7,16,24,2,256]{4,2,3,0,1:T(8,128)(2,1)} %bitcast.32) | data formatting | bytes 5505024 | tf_op jit(solution)/shard_map/all_to_all | solution.py:104
  343.4 6.8 %reshape.396 = bf16[7,768,256]{2,1,0:T(8,128)(2,1)} reshape(bf16[7,16,24,2,256]{4,3,2,1,0:T(2,128)(2,1)} %copy.42) | data formatting | bytes 5505024 | tf_op jit(solution)/shard_map/reshape | solution.py:105
  350.2 9.1 %convert_bitcast_fusion = bf16[7,1440,256]{2,1,0:T(8,128)(2,1)} fusion(bf16[7,768,256]{2,1,0:T(8,128)(2,1)} %reshape.396, bf16[768,1440]{1,0:T(8,128)(2,1)} %convert_element_type.90), kind=kOutput, calls=%fused_computation.16 | convolution fusion | flops 3966197760 | bytes 10125312 | tf_op jit(solution)/shard_map/sqc,qk->skc/dot_general | solution.py:106
  (52 shorter events, 45.7 us)
Async XLA Ops:
  0.0 186.9 %copy-start = (bf16[24,96,384]{2,1,0:T(8,128)(2,1)S(1)}, bf16[24,96,384]{2,1,0:T(8,128)(2,1)}, u32[]{:S(2)}) copy-start(bf16[24,96,384]{2,1,0:T(8,128)(2,1)} %param.10) | copy-start | bytes 5308420
  22.4 6.0 %copy-start.3 = (s32[16]{0:T(128)S(1)}, s32[16]{0:T(128)}, u32[]{:S(2)}) copy-start(s32[16]{0:T(128)} %param.8) | copy-start | bytes 196
  98.5 17.5 %copy-start.1 = (f32[384,256]{1,0:T(8,128)S(1)}, f32[384,256]{1,0:T(8,128)}, u32[]{:S(2)}) copy-start(f32[384,256]{1,0:T(8,128)} %param.12) | copy-start | bytes 1179652
  98.5 78.3 %all-to-all-start = ((bf16[16,7,24,2,256]{4,3,2,1,0:T(2,128)(2,1)}), bf16[16,7,24,2,256]{4,3,2,1,0:T(2,128)(2,1)}, u32[]{:S(2)}, u32[]{:S(2)}) async-start(bf16[16,7,24,2,256]{4,3,2,1,0:T(2,128)(2,1)} %fusion.31), calls=%async_computation | async-start | bytes 5505024 | tf_op jit(solution)/shard_map/all_to_all | solution.py:76
  180.6 4.0 %copy-start.4 = (f32[96]{0:T(128)S(1)}, f32[96]{0:T(128)}, u32[]{:S(2)}) copy-start(f32[96]{0:T(128)} %param.11) | copy-start | bytes 1156
  216.6 14.6 %copy-start.2 = (bf16[256,256]{1,0:T(8,128)(2,1)S(1)}, bf16[256,256]{1,0:T(8,128)(2,1)}, u32[]{:S(2)}) copy-start(bf16[256,256]{1,0:T(8,128)(2,1)} %param.13) | copy-start | bytes 393220
  271.3 66.3 %all-to-all-start.1 = ((bf16[112,24,2,256]{3,1,2,0:T(8,128)(2,1)}), bf16[112,24,2,256]{3,1,2,0:T(8,128)(2,1)}, u32[]{:S(2)}, u32[]{:S(2)}) async-start(bf16[112,24,2,256]{3,1,2,0:T(8,128)(2,1)} %select_select_fusion), calls=%async_computation.1 | async-start | bytes 5505024 | tf_op jit(solution)/shard_map/all_to_all | solution.py:104
